TPU v7x, 32 devices: a whole 2x2x4 slice. The times are simulated.
32 devices in a mesh: section: 2 (over x), tensor: 8 (over z, core), dp: 2 (over y).
Axes of the slice: x: 2, y: 2, z: 4, core: 2. Of those that a mesh axis runs over, the one named last changes fastest.
Arguments:
- dec_queries: bfloat16 [2, 4, 512, 8192], P('section', 'dp', None, 'tensor'), may hold values from -8 to 8
- enc_keys: bfloat16 [2, 4, 512, 8192], P('section', 'dp', None, 'tensor'), may hold values from -4 to 4
- enc_values: bfloat16 [2, 4, 512, 8192], P('section', 'dp', None, 'tensor'), may hold values from -4 to 4
- out_grad: bfloat16 [2, 4, 512, 8192], P('section', 'dp', None, 'tensor'), may hold values from -15 to 15
- key_weight: bfloat16 [2, 1024, 8192], P('section', None, 'tensor'), may hold values from -0.1875 to 0.1875
- value_weight: bfloat16 [2, 1024, 8192], P('section', None, 'tensor'), may hold values from -0.1875 to 0.1875
- enc_hidden: float32 [4, 512, 1024], P('dp', 'section', 'tensor'), may hold values from -2 to 2, as said below
- enc_gain: float32 [1024], P('tensor'), may hold values from 0.1 to 1.9
Outputs:
- enc_input_grad: float32 [4, 512, 1024], P('dp', 'section', 'tensor')
Inputs may be any that keep to these rules, and one draw needn't show every extreme that they name: `enc_hidden`: every entry's magnitude is at least 0.25.
All inputs are finite; a program needn't handle non-finite values.
Results may differ from a plain program's by a relative error of at most 0.0041.
Values sent between devices are 32-bit elements; how exact they have to be, the bound alone decides.
A program may use at most 128 MiB of HBM per device.

v0:
```python
import jax
import jax.numpy as jnp
from jax import lax
from jax.sharding import PartitionSpec as P

D = 1024
DK = 128
epsilon = 1e-06


def per_device(
    dec_queries, enc_keys, enc_values, out_grad, key_weight, value_weight, enc_hidden, enc_gain
):
    seqs_here = dec_queries.shape[1]
    dec_len = dec_queries.shape[2]
    hidden_here = dec_queries.shape[3]
    enc_len = enc_keys.shape[2]
    heads_here = hidden_here // DK
    model_width = key_weight.shape[1]
    square_total = lax.psum(jnp.sum(enc_hidden * enc_hidden, axis=-1), "tensor")
    query_heads = dec_queries[0].reshape(seqs_here, dec_len, heads_here, DK)
    key_heads = enc_keys[0].reshape(seqs_here, enc_len, heads_here, DK)
    value_heads = enc_values[0].reshape(seqs_here, enc_len, heads_here, DK)
    grad_heads = out_grad[0].reshape(seqs_here, dec_len, heads_here, DK)
    scores = jnp.einsum(
        "bqhd,bkhd->bhqk", query_heads, key_heads, preferred_element_type=jnp.float32
    )
    shifted = jnp.exp(scores - jnp.max(scores, axis=-1, keepdims=True))
    attn_probs = shifted / jnp.sum(shifted, axis=-1, keepdims=True)
    probs_low = attn_probs.astype(jnp.bfloat16)
    attended = jnp.einsum(
        "bhqk,bkhd->bqhd", probs_low, value_heads, preferred_element_type=jnp.float32
    )
    row_dot = jnp.sum(grad_heads.astype(jnp.float32) * attended, axis=-1)
    value_grad = jnp.einsum(
        "bhqk,bqhd->bkhd", probs_low, grad_heads, preferred_element_type=jnp.float32
    ).astype(jnp.bfloat16)
    prob_grad = jnp.einsum(
        "bqhd,bkhd->bhqk", grad_heads, value_heads, preferred_element_type=jnp.float32
    )
    score_low = (attn_probs * (prob_grad - jnp.transpose(row_dot, (0, 2, 1))[..., None])).astype(
        jnp.bfloat16
    )
    key_grad = jnp.einsum(
        "bhqk,bqhd->bkhd", score_low, query_heads, preferred_element_type=jnp.float32
    ).astype(jnp.bfloat16)
    flat_rows = seqs_here * enc_len
    partial_value = jnp.einsum(
        "th,dh->td",
        key_grad.reshape(flat_rows, hidden_here),
        key_weight[0],
        preferred_element_type=jnp.float32,
    )
    partial_value = partial_value + jnp.einsum(
        "th,dh->td",
        value_grad.reshape(flat_rows, hidden_here),
        value_weight[0],
        preferred_element_type=jnp.float32,
    )
    partial_value = partial_value.reshape(seqs_here, enc_len, model_width)
    head_part = lax.psum_scatter(partial_value, "tensor", scatter_dimension=2, tiled=True)
    enc_grad = lax.psum_scatter(head_part, "section", scatter_dimension=1, tiled=True)
    scaled = enc_gain * enc_grad
    cross_local = jnp.sum(scaled * enc_hidden, axis=-1)
    cross_total = lax.psum(cross_local, "tensor")
    inverse = lax.rsqrt(square_total / D + epsilon)
    return (
        scaled * inverse[..., None]
        - enc_hidden * (cross_total * inverse * inverse * inverse / D)[..., None]
    )


def solution(mesh):
    return jax.shard_map(
        per_device,
        mesh=mesh,
        in_specs=(
            P("section", "dp", None, "tensor"),
            P("section", "dp", None, "tensor"),
            P("section", "dp", None, "tensor"),
            P("section", "dp", None, "tensor"),
            P("section", None, "tensor"),
            P("section", None, "tensor"),
            P("dp", "section", "tensor"),
            P("tensor"),
        ),
        out_specs=P("dp", "section", "tensor"),
        check_vma=False,
    )
```

profile of v0, /device:TPU:0, one launch (start us, length us, event | category | flops | bytes accessed | tf_op | source)
XLA Modules:
  0.0 159.6 jit_solution(9555363609104835648)
XLA Ops:
  6.5 0.0 copy-start
  6.5 0.0 reduce-scatter.3.cloned.1.call-start
  6.5 3.7 %copy.40 = bf16[128,8,8,128]{3,2,1,0:T(8,128)(2,1)} copy(bf16[128,8,8,128]{3,1,2,0:T(8,128)(2,1)} %bitcast.55) | data formatting | bytes 4194304
  10.3 0.0 copy-done.3
  10.3 2.0 %copy.41 = bf16[128,8,8,128]{3,2,1,0:T(8,128)(2,1)} copy(bf16[128,8,8,128]{3,1,2,0:T(8,128)(2,1)S(1)} %bitcast.56) | data formatting | bytes 4194304
  12.2 3.9 %copy.39 = bf16[1,2,512,1024]{2,3,1,0:T(8,128)(2,1)} copy(bf16[1,2,512,1024]{3,2,1,0:T(8,128)(2,1)} %param.10) | data formatting | bytes 4194304 | tf_op jit(solution)/shard_map/reshape;squeeze | solution.py:23
  16.2 3.9 %copy.21 = bf16[1,2,512,1024]{2,3,1,0:T(8,128)(2,1)} copy(bf16[1,2,512,1024]{3,2,1,0:T(8,128)(2,1)} %param.11) | data formatting | bytes 4194304 | tf_op args[3]
  20.1 10.7 %fusion.29 = (f32[2,8,512]{2,1,0:T(8,128)S(1)}, f32[2,8,512,512]{2,3,1,0:T(8,128)}) fusion(bf16[2,512,8,128]{3,2,1,0:T(8,128)(2,1)} %bitcast.60, bf16[2,512,8,128]{3,2,1,0:T(8,128)(2,1)} %bitcast.57), kind=kOutput, calls=%fused_computation.31 | convolution fusion | flops 1082130944 | bytes 21004288 | tf_op jit(solution)/shard_map/sub | solution.py:28
  30.8 6.8 %fusion.3 = bf16[2,8,512,512]{2,3,1,0:T(8,128)(2,1)S(1)} fusion(f32[2,8,512,512]{2,3,1,0:T(8,128)} %get-tuple-element.12, f32[2,8,512]{2,1,0:T(8,128)S(1)} %get-tuple-element.11), kind=kLoop, calls=%fused_computation.6 | loop fusion | flops 8388608 | bytes 25198592 | tf_op jit(solution)/shard_map/convert_element_type | solution.py:30
  37.6 0.0 copy-done.2
  37.6 0.0 copy-start.1
  37.6 2.3 %convert_bitcast_fusion = bf16[2,512,8,128]{3,1,2,0:T(8,128)(2,1)S(1)} fusion(bf16[2,8,512,512]{2,3,1,0:T(8,128)(2,1)S(1)} %fusion.3, bf16[2,512,8,128]{1,3,2,0:T(8,128)(2,1)S(1)} %bitcast.52), kind=kOutput, calls=%fused_computation.20 | convolution fusion | flops 1074790400 | bytes 12582912 | tf_op jit(solution)/shard_map/bhqk,bqhd->bkhd/dot_general | solution.py:35
  40.0 0.0 copy-done.1
  40.0 1.3 fusion.6
  41.3 2.7 %copy.32 = bf16[2,512,8,128]{3,2,1,0:T(8,128)(2,1)} copy(bf16[2,512,8,128]{3,1,2,0:T(8,128)(2,1)S(1)} %convert_bitcast_fusion) | data formatting | bytes 4194304 | tf_op jit(solution)/shard_map/convert_element_type | solution.py:37
  44.0 11.6 %convert_bitcast_fusion.1 = bf16[2,512,8,128]{3,1,2,0:T(8,128)(2,1)} fusion(f32[2,8,512]{2,1,0:T(8,128)S(1)} %bitcast.62, f32[2,8,512,512]{2,3,1,0:T(8,128)} %get-tuple-element.12, f32[2,8,512]{2,1,0:T(8,128)S(1)} %get-tuple-element.11, bf16[2,512,8,128]{1,3,2,0:T(8,128)(2,1)} %bitcast.49, bf16[2,512,8,128]{1,3,2,0:T(8,128)(2,1)} %bitcast.51, ...), kind=kOutput, calls=%fused_computation.21 | convolution fusion | flops 2165309440 | bytes 25231360 | tf_op jit(solution)/shard_map/bhqk,bqhd->bkhd/dot_general | solution.py:44
  55.5 3.1 %copy.30 = bf16[2,512,8,128]{3,2,1,0:T(8,128)(2,1)S(1)} copy(bf16[2,512,8,128]{3,1,2,0:T(8,128)(2,1)} %convert_bitcast_fusion.1) | data formatting | bytes 4194304 | tf_op jit(solution)/shard_map/convert_element_type | solution.py:46
  58.6 0.0 copy-done
  58.7 0.0 copy-done.4
  58.7 0.0 copy-start.7
  58.7 2.4 %fusion.7 = f32[1024,1024]{1,0:T(8,128)S(1)} fusion(bf16[128,8,8,128]{3,2,1,0:T(8,128)(2,1)S(1)} %bitcast.59, bf16[1,1024,1024]{2,1,0:T(8,128)(2,1)S(1)} %copy-done), kind=kOutput, calls=%fused_computation.10 | convolution fusion | flops 2147483648 | bytes 8388608 | tf_op jit(solution)/shard_map/th,dh->td/dot_general | solution.py:54
  61.0 0.0 copy-done.7
  61.1 4.3 %fusion.17 = f32[1024,1024]{1,0:T(8,128)} fusion(f32[1024,1024]{1,0:T(8,128)S(1)} %fusion.7, bf16[1,1024,1024]{2,1,0:T(8,128)(2,1)S(1)} %copy-done.7, bf16[128,8,8,128]{3,2,1,0:T(8,128)(2,1)S(1)} %bitcast.61), kind=kOutput, calls=%fused_computation.22 | convolution fusion | flops 2148532224 | bytes 12582912 | tf_op jit(solution)/shard_map/th,dh->td/dot_general | solution.py:48
  65.3 0.0 reduce-scatter.3.cloned.1.call-update
  65.4 0.0 reduce-scatter.5.cloned.1.call-start
  65.4 52.8 %reduce-scatter.3.cloned.1.call-done = f32[2,512,128]{2,1,0:T(8,128)} async-done(((f32[2,512,1024]{2,1,0:T(8,128)}), f32[2,512,128]{2,1,0:T(8,128)}) %reduce-scatter.3.cloned.1.call-update) | async-done | bytes 524304 | tf_op jit(solution)/shard_map/reduce_scatter | solution.py:61
  118.2 0.0 reduce-scatter.5.cloned.1.call-update
  118.2 15.4 %reduce-scatter.5.cloned.1.call-done = f32[2,256,128]{2,1,0:T(8,128)} async-done(((f32[2,512,128]{2,1,0:T(8,128)}), f32[2,256,128]{2,1,0:T(8,128)}) %reduce-scatter.5.cloned.1.call-update) | async-done | bytes 262160 | tf_op jit(solution)/shard_map/reduce_scatter | solution.py:62
  133.6 0.0 copy-done.5
  133.6 1.2 multiply_reduce_fusion.1
  134.7 16.2 %all-reduce = (f32[2,256]{1,0:T(2,128)S(1)}, f32[2,256]{1,0:T(2,128)S(1)}) all-reduce(f32[2,256]{1,0:T(2,128)S(1)} %get-tuple-element.6, f32[2,256]{1,0:T(2,128)S(1)} %get-tuple-element.5), channel_id=1, replica_groups=mesh['section'=2,'tensor'=8,'dp'=2] {'tensor'}, use_global_device_ids=true, to_apply=%region_8.0 | all-reduce | flops 1024 | bytes 8192 | tf_op jit(solution)/shard_map/psum | solution.py:65
  150.9 1.9 %multiply_subtract_fusion = f32[2,256,128]{2,1,0:T(8,128)} fusion(f32[2,256,128]{2,1,0:T(8,128)S(1)} %copy-done.5, f32[2,256,128]{2,1,0:T(8,128)} %reduce-scatter.5.cloned.1.call-done, f32[2,256]{1,0:T(2,128)S(1)} %get-tuple-element.10, f32[2,256]{1,0:T(2,128)S(1)} %get-tuple-element.9, f32[128]{0:T(128)S(1)} %copy-done.6), kind=kLoop, calls=%fused_computation.25 | loop fusion | flops 262144 | bytes 791040 | tf_op jit(solution)/shard_map/sub | solution.py:68
  (7 shorter events, 0.0 us)
Async XLA Ops:
  6.5 52.1 %copy-start = (bf16[1,1024,1024]{2,1,0:T(8,128)(2,1)S(1)}, bf16[1,1024,1024]{2,1,0:T(8,128)(2,1)}, u32[]{:S(2)}) copy-start(bf16[1,1024,1024]{2,1,0:T(8,128)(2,1)} %param.13) | copy-start | bytes 6291460
  6.5 111.6 %reduce-scatter.3.cloned.1.call-start = ((), (), s32[]{:S(2)}) async-start(), calls=%async_computation.2 | async-start | bytes 4718592 | tf_op jit(solution)/shard_map/reduce_scatter | solution.py:61
  6.5 3.7 %copy-start.3 = (bf16[1,2,512,1024]{3,2,1,0:T(8,128)(2,1)S(1)}, bf16[1,2,512,1024]{3,2,1,0:T(8,128)(2,1)}, u32[]{:S(2)}) copy-start(bf16[1,2,512,1024]{3,2,1,0:T(8,128)(2,1)} %param.9) | copy-start | bytes 6291460
  30.8 6.9 %copy-start.2 = (bf16[1,2,512,1024]{2,3,1,0:T(8,128)(2,1)S(1)}, bf16[1,2,512,1024]{2,3,1,0:T(8,128)(2,1)}, u32[]{:S(2)}) copy-start(bf16[1,2,512,1024]{2,3,1,0:T(8,128)(2,1)} %copy.21) | copy-start | bytes 6291460
  37.6 2.4 %copy-start.1 = (bf16[1,2,512,1024]{2,3,1,0:T(8,128)(2,1)S(1)}, bf16[1,2,512,1024]{2,3,1,0:T(8,128)(2,1)}, u32[]{:S(2)}) copy-start(bf16[1,2,512,1024]{2,3,1,0:T(8,128)(2,1)} %copy.39) | copy-start | bytes 6291460
  55.5 3.1 %copy-start.4 = (bf16[2,512,8,128]{3,2,1,0:T(8,128)(2,1)S(1)}, bf16[2,512,8,128]{3,2,1,0:T(8,128)(2,1)}, u32[]{:S(2)}) copy-start(bf16[2,512,8,128]{3,2,1,0:T(8,128)(2,1)} %copy.32) | copy-start | bytes 6291460
  58.7 2.4 %copy-start.7 = (bf16[1,1024,1024]{2,1,0:T(8,128)(2,1)S(1)}, bf16[1,1024,1024]{2,1,0:T(8,128)(2,1)}, u32[]{:S(2)}) copy-start(bf16[1,1024,1024]{2,1,0:T(8,128)(2,1)} %param.12) | copy-start | bytes 6291460
  65.3 68.2 %copy-start.5 = (f32[2,256,128]{2,1,0:T(8,128)S(1)}, f32[2,256,128]{2,1,0:T(8,128)}, u32[]{:S(2)}) copy-start(f32[2,256,128]{2,1,0:T(8,128)} %param.14) | copy-start | bytes 786436
  65.3 68.2 %copy-start.6 = (f32[128]{0:T(128)S(1)}, f32[128]{0:T(128)}, u32[]{:S(2)}) copy-start(f32[128]{0:T(128)} %param.15) | copy-start | bytes 1540
  65.4 68.2 %reduce-scatter.5.cloned.1.call-start = ((), (), s32[]{:S(2)}) async-start(), calls=%async_computation.3 | async-start | bytes 786432 | tf_op jit(solution)/shard_map/reduce_scatter | solution.py:62
Sparse Core Ops, SparseCore 0:
  65.5 52.6 reduce-scatter.2
  120.4 13.0 reduce-scatter.4
where the time goes:
time: 160 us
  waiting for transfers between devices  68.1 us (43%)
  matrix products  32.5 us (20%)
  local copies, waits for them, and re-layouts  19.4 us (12%)
  blocking collectives  16.2 us (10%)
  between operations  13.5 us (8%)
  other arithmetic  9.88 us (6%)
    reduce_scatter x1, waiting for transfers between devices, per_device(): lax.psum_scatter(partial_value, 'tensor', scatter_dimension=2, tiled=True)  52.8 us
    psum x1, blocking collectives, per_device(): cross_total = lax.psum(cross_local, 'tensor')  16.2 us
    reduce_scatter x1, waiting for transfers between devices, per_device(): lax.psum_scatter(head_part, 'section', scatter_dimension=1, tiled=True)  15.4 us
    dot_general x1, matrix products, per_device(): jnp.einsum('bhqk,bqhd->bkhd', score_low, query_heads, preferred_element_t...  11.6 us
    sub x1, matrix products, per_device(): shifted = jnp.exp(scores - jnp.max(scores, axis=-1, keepdims=True))  10.7 us
    unnamed x19, local copies, waits for them, and re-layouts  9.66 us
    convert_element_type x1, other arithmetic, per_device(): probs_low = attn_probs.astype(jnp.bfloat16)  6.84 us
    dot_general x1, matrix products, per_device(): jnp.einsum('th,dh->td', key_grad.reshape(flat_rows, hidden_here), key_wei...  4.29 us
  transfers between devices with their start and end apart: 2, of which 2 were waited for; matrix products, arithmetic and copies ran while one was open for 0% of the time, Pallas kernels for 0%

commit v1 on v0

--- a/solution.py
+++ b/solution.py
@@ -2,6 +2,7 @@
 import jax.numpy as jnp
 from jax import lax
 from jax.sharding import PartitionSpec as P
+from jax.lax import all_gather
 
 D = 1024
 DK = 128
@@ -62,7 +63,7 @@
     enc_grad = lax.psum_scatter(head_part, "section", scatter_dimension=1, tiled=True)
     scaled = enc_gain * enc_grad
     cross_local = jnp.sum(scaled * enc_hidden, axis=-1)
-    cross_total = lax.psum(cross_local, "tensor")
+    cross_total = all_gather(cross_local, axis_name="tensor").sum(axis=0)
     inverse = lax.rsqrt(square_total / D + epsilon)
     return (
         scaled * inverse[..., None]

time: 160 us -> 173 us (1.081)
  blocking collectives: 16.2 us -> 29 us
    all_gather x0 -> x1, blocking collectives: none -> 12.8 us  [per_device(): cross_total = all_gather(cross_local, axis_name='tensor').sum(axis=0)]
where the time goes in v1:
time: 173 us; the launch traced here: 172 us
  waiting for transfers between devices  68.1 us (39%)
  matrix products  32.5 us (19%)
  blocking collectives  29 us (17%)
  local copies, waits for them, and re-layouts  19.4 us (11%)
  between operations  13.5 us (8%)
  other arithmetic  9.9 us (6%)
    reduce_scatter x1, waiting for transfers between devices, per_device(): lax.psum_scatter(partial_value, 'tensor', scatter_dimension=2, tiled=True)  52.8 us
    psum x1, blocking collectives, per_device(): square_total = lax.psum(jnp.sum(enc_hidden * enc_hidden, axis=-1), 'tensor')  16.2 us
    reduce_scatter x1, waiting for transfers between devices, per_device(): lax.psum_scatter(head_part, 'section', scatter_dimension=1, tiled=True)  15.4 us
    all_gather x1, blocking collectives, per_device(): cross_total = all_gather(cross_local, axis_name='tensor').sum(axis=0)  12.8 us
    dot_general x1, matrix products, per_device(): jnp.einsum('bhqk,bqhd->bkhd', score_low, query_heads, preferred_element_t...  11.6 us
    sub x1, matrix products, per_device(): shifted = jnp.exp(scores - jnp.max(scores, axis=-1, keepdims=True))  10.7 us
    unnamed x19, local copies, waits for them, and re-layouts  9.66 us
    convert_element_type x1, other arithmetic, per_device(): probs_low = attn_probs.astype(jnp.bfloat16)  6.84 us
  transfers between devices with their start and end apart: 2, of which 2 were waited for; matrix products, arithmetic and copies ran while one was open for 0% of the time, Pallas kernels for 0%

profile of v1, /device:TPU:0, one launch (start us, length us, event | category | flops | bytes accessed | tf_op | source)
XLA Modules:
  0.0 172.4 jit_solution(14212311878776878342)
XLA Ops:
  6.5 0.0 copy-start
  6.5 0.0 reduce-scatter.3.cloned.1.call-start
  6.5 3.7 %copy.40 = bf16[128,8,8,128]{3,2,1,0:T(8,128)(2,1)} copy(bf16[128,8,8,128]{3,1,2,0:T(8,128)(2,1)} %bitcast.56) | data formatting | bytes 4194304
  10.3 0.0 copy-done.3
  10.3 2.0 %copy.41 = bf16[128,8,8,128]{3,2,1,0:T(8,128)(2,1)} copy(bf16[128,8,8,128]{3,1,2,0:T(8,128)(2,1)S(1)} %bitcast.57) | data formatting | bytes 4194304
  12.2 3.9 %copy.39 = bf16[1,2,512,1024]{2,3,1,0:T(8,128)(2,1)} copy(bf16[1,2,512,1024]{3,2,1,0:T(8,128)(2,1)} %param.10) | data formatting | bytes 4194304 | tf_op jit(solution)/shard_map/reshape;squeeze | solution.py:24
  16.2 3.9 %copy.21 = bf16[1,2,512,1024]{2,3,1,0:T(8,128)(2,1)} copy(bf16[1,2,512,1024]{3,2,1,0:T(8,128)(2,1)} %param.11) | data formatting | bytes 4194304 | tf_op args[3]
  20.1 10.7 %fusion.29 = (f32[2,8,512]{2,1,0:T(8,128)S(1)}, f32[2,8,512,512]{2,3,1,0:T(8,128)}) fusion(bf16[2,512,8,128]{3,2,1,0:T(8,128)(2,1)} %bitcast.61, bf16[2,512,8,128]{3,2,1,0:T(8,128)(2,1)} %bitcast.58), kind=kOutput, calls=%fused_computation.31 | convolution fusion | flops 1082130944 | bytes 21004288 | tf_op jit(solution)/shard_map/sub | solution.py:29
  30.8 6.8 %fusion.3 = bf16[2,8,512,512]{2,3,1,0:T(8,128)(2,1)S(1)} fusion(f32[2,8,512,512]{2,3,1,0:T(8,128)} %get-tuple-element.10, f32[2,8,512]{2,1,0:T(8,128)S(1)} %get-tuple-element.9), kind=kLoop, calls=%fused_computation.6 | loop fusion | flops 8388608 | bytes 25198592 | tf_op jit(solution)/shard_map/convert_element_type | solution.py:31
  37.6 0.0 copy-done.2
  37.6 0.0 copy-start.1
  37.6 2.3 %convert_bitcast_fusion = bf16[2,512,8,128]{3,1,2,0:T(8,128)(2,1)S(1)} fusion(bf16[2,8,512,512]{2,3,1,0:T(8,128)(2,1)S(1)} %fusion.3, bf16[2,512,8,128]{1,3,2,0:T(8,128)(2,1)S(1)} %bitcast.53), kind=kOutput, calls=%fused_computation.20 | convolution fusion | flops 1074790400 | bytes 12582912 | tf_op jit(solution)/shard_map/bhqk,bqhd->bkhd/dot_general | solution.py:36
  40.0 0.0 copy-done.1
  40.0 1.3 fusion.6
  41.3 2.7 %copy.32 = bf16[2,512,8,128]{3,2,1,0:T(8,128)(2,1)} copy(bf16[2,512,8,128]{3,1,2,0:T(8,128)(2,1)S(1)} %convert_bitcast_fusion) | data formatting | bytes 4194304 | tf_op jit(solution)/shard_map/convert_element_type | solution.py:38
  44.0 11.6 %convert_bitcast_fusion.1 = bf16[2,512,8,128]{3,1,2,0:T(8,128)(2,1)} fusion(f32[2,8,512]{2,1,0:T(8,128)S(1)} %bitcast.63, f32[2,8,512,512]{2,3,1,0:T(8,128)} %get-tuple-element.10, f32[2,8,512]{2,1,0:T(8,128)S(1)} %get-tuple-element.9, bf16[2,512,8,128]{1,3,2,0:T(8,128)(2,1)} %bitcast.50, bf16[2,512,8,128]{1,3,2,0:T(8,128)(2,1)} %bitcast.52, ...), kind=kOutput, calls=%fused_computation.21 | convolution fusion | flops 2165309440 | bytes 25231360 | tf_op jit(solution)/shard_map/bhqk,bqhd->bkhd/dot_general | solution.py:45
  55.5 3.1 %copy.30 = bf16[2,512,8,128]{3,2,1,0:T(8,128)(2,1)S(1)} copy(bf16[2,512,8,128]{3,1,2,0:T(8,128)(2,1)} %convert_bitcast_fusion.1) | data formatting | bytes 4194304 | tf_op jit(solution)/shard_map/convert_element_type | solution.py:47
  58.6 0.0 copy-done
  58.7 0.0 copy-done.4
  58.7 0.0 copy-start.7
  58.7 2.4 %fusion.7 = f32[1024,1024]{1,0:T(8,128)S(1)} fusion(bf16[128,8,8,128]{3,2,1,0:T(8,128)(2,1)S(1)} %bitcast.60, bf16[1,1024,1024]{2,1,0:T(8,128)(2,1)S(1)} %copy-done), kind=kOutput, calls=%fused_computation.10 | convolution fusion | flops 2147483648 | bytes 8388608 | tf_op jit(solution)/shard_map/th,dh->td/dot_general | solution.py:55
  61.0 0.0 copy-done.7
  61.1 4.3 %fusion.17 = f32[1024,1024]{1,0:T(8,128)} fusion(f32[1024,1024]{1,0:T(8,128)S(1)} %fusion.7, bf16[1,1024,1024]{2,1,0:T(8,128)(2,1)S(1)} %copy-done.7, bf16[128,8,8,128]{3,2,1,0:T(8,128)(2,1)S(1)} %bitcast.62), kind=kOutput, calls=%fused_computation.22 | convolution fusion | flops 2148532224 | bytes 12582912 | tf_op jit(solution)/shard_map/th,dh->td/dot_general | solution.py:49
  65.3 0.0 reduce-scatter.3.cloned.1.call-update
  65.4 0.0 reduce-scatter.5.cloned.1.call-start
  65.4 52.8 %reduce-scatter.3.cloned.1.call-done = f32[2,512,128]{2,1,0:T(8,128)} async-done(((f32[2,512,1024]{2,1,0:T(8,128)}), f32[2,512,128]{2,1,0:T(8,128)}) %reduce-scatter.3.cloned.1.call-update) | async-done | bytes 524304 | tf_op jit(solution)/shard_map/reduce_scatter | solution.py:62
  118.2 0.0 reduce-scatter.5.cloned.1.call-update
  118.2 15.4 %reduce-scatter.5.cloned.1.call-done = f32[2,256,128]{2,1,0:T(8,128)} async-done(((f32[2,512,128]{2,1,0:T(8,128)}), f32[2,256,128]{2,1,0:T(8,128)}) %reduce-scatter.5.cloned.1.call-update) | async-done | bytes 262160 | tf_op jit(solution)/shard_map/reduce_scatter | solution.py:63
  133.6 1.2 multiply_reduce_fusion.1
  134.7 16.2 %psum.7 = f32[2,256]{1,0:T(2,128)S(1)} all-reduce(f32[2,256]{1,0:T(2,128)S(1)} %get-tuple-element.5), channel_id=1, replica_groups=mesh['section'=2,'tensor'=8,'dp'=2] {'tensor'}, use_global_device_ids=true, to_apply=%region_6.0 | all-reduce | flops 512 | bytes 4096 | tf_op jit(solution)/shard_map/psum | solution.py:21
  150.9 12.8 %all-gather.1 = f32[8,2,256]{2,1,0:T(2,128)S(1)} all-gather(f32[1,2,256]{2,1,0:T(2,128)S(1)} %bitcast.64), channel_id=2, replica_groups=mesh['section'=2,'tensor'=8,'dp'=2] {'tensor'}, dimensions={0}, use_global_device_ids=true | all-gather | bytes 18432 | tf_op jit(solution)/shard_map/all_gather | solution.py:66
  163.7 1.9 %multiply_subtract_fusion = f32[2,256,128]{2,1,0:T(8,128)} fusion(f32[2,256,128]{2,1,0:T(8,128)S(1)} %copy-done.5, f32[2,256,128]{2,1,0:T(8,128)} %reduce-scatter.5.cloned.1.call-done, f32[2,256]{1,0:T(2,128)S(1)} %get-tuple-element.8, f32[2,256]{1,0:T(2,128)S(1)} %get-tuple-element.7, f32[128]{0:T(128)S(1)} %copy-done.6), kind=kLoop, calls=%fused_computation.25 | loop fusion | flops 262144 | bytes 791040 | tf_op jit(solution)/shard_map/sub | solution.py:69
  (9 shorter events, 0.0 us)
Async XLA Ops:
  6.5 52.1 %copy-start = (bf16[1,1024,1024]{2,1,0:T(8,128)(2,1)S(1)}, bf16[1,1024,1024]{2,1,0:T(8,128)(2,1)}, u32[]{:S(2)}) copy-start(bf16[1,1024,1024]{2,1,0:T(8,128)(2,1)} %param.13) | copy-start | bytes 6291460
  6.5 111.6 %reduce-scatter.3.cloned.1.call-start = ((), (), s32[]{:S(2)}) async-start(), calls=%async_computation.2 | async-start | bytes 4718592 | tf_op jit(solution)/shard_map/reduce_scatter | solution.py:62
  6.5 3.7 %copy-start.3 = (bf16[1,2,512,1024]{3,2,1,0:T(8,128)(2,1)S(1)}, bf16[1,2,512,1024]{3,2,1,0:T(8,128)(2,1)}, u32[]{:S(2)}) copy-start(bf16[1,2,512,1024]{3,2,1,0:T(8,128)(2,1)} %param.9) | copy-start | bytes 6291460
  30.8 6.9 %copy-start.2 = (bf16[1,2,512,1024]{2,3,1,0:T(8,128)(2,1)S(1)}, bf16[1,2,512,1024]{2,3,1,0:T(8,128)(2,1)}, u32[]{:S(2)}) copy-start(bf16[1,2,512,1024]{2,3,1,0:T(8,128)(2,1)} %copy.21) | copy-start | bytes 6291460
  37.6 2.4 %copy-start.1 = (bf16[1,2,512,1024]{2,3,1,0:T(8,128)(2,1)S(1)}, bf16[1,2,512,1024]{2,3,1,0:T(8,128)(2,1)}, u32[]{:S(2)}) copy-start(bf16[1,2,512,1024]{2,3,1,0:T(8,128)(2,1)} %copy.39) | copy-start | bytes 6291460
  55.5 3.1 %copy-start.4 = (bf16[2,512,8,128]{3,2,1,0:T(8,128)(2,1)S(1)}, bf16[2,512,8,128]{3,2,1,0:T(8,128)(2,1)}, u32[]{:S(2)}) copy-start(bf16[2,512,8,128]{3,2,1,0:T(8,128)(2,1)} %copy.32) | copy-start | bytes 6291460
  58.7 2.4 %copy-start.7 = (bf16[1,1024,1024]{2,1,0:T(8,128)(2,1)S(1)}, bf16[1,1024,1024]{2,1,0:T(8,128)(2,1)}, u32[]{:S(2)}) copy-start(bf16[1,1024,1024]{2,1,0:T(8,128)(2,1)} %param.12) | copy-start | bytes 6291460
  65.3 68.2 %copy-start.5 = (f32[2,256,128]{2,1,0:T(8,128)S(1)}, f32[2,256,128]{2,1,0:T(8,128)}, u32[]{:S(2)}) copy-start(f32[2,256,128]{2,1,0:T(8,128)} %param.14) | copy-start | bytes 786436
  65.3 68.2 %copy-start.6 = (f32[128]{0:T(128)S(1)}, f32[128]{0:T(128)}, u32[]{:S(2)}) copy-start(f32[128]{0:T(128)} %param.15) | copy-start | bytes 1540
  65.4 68.2 %reduce-scatter.5.cloned.1.call-start = ((), (), s32[]{:S(2)}) async-start(), calls=%async_computation.3 | async-start | bytes 786432 | tf_op jit(solution)/shard_map/reduce_scatter | solution.py:63
Sparse Core Ops, SparseCore 0:
  65.5 52.6 reduce-scatter.2
  120.4 13.0 reduce-scatter.4
